TPU v7x, 128 devices: a whole 4x4x4 slice. The times are simulated.
128 devices in a mesh: seg: 128 (over y, x, z, core).
Axes of the slice: x: 4, y: 4, z: 4, core: 2. Of those that a mesh axis runs over, the one named last changes fastest.
Arguments:
- strain: bfloat16 [3, 256, 3, 2, 65536], P(None, 'seg'), may hold values from -6 to 6
- valid: int32 [256], P('seg'), may hold values from 0 to 1, as said below
- intersection: float32 [3, 65536], replicated, may hold values from -1 to 1, as said below
- notch: int32 [65536], replicated, may hold values from 0 to 1, as said below
Outputs:
- contribution: float32 [3, 65536], P(None, 'seg')
- broadband: float32 [3, 2], replicated
Inputs may be any that keep to these rules, and one draw needn't show every extreme that they name: At least one segment is valid. `intersection`: never zero. `notch`: at least one bin is kept.
All inputs are finite; a program needn't handle non-finite values.
Results may differ from a plain program's by a relative error of at most 0.011.
Values sent between devices are 32-bit elements; how exact they have to be, the bound alone decides.
A program may use at most 256 MiB of HBM per device.

v0:
```python
import functools
import math

import jax
import jax.numpy as jnp
from jax import lax
from jax.sharding import Mesh
from jax.sharding import PartitionSpec as P

FA = 256
FB = 256
SEG = ("seg_0", "seg_1", "seg_2", "seg_3")


baseline_pairs = ((0, 1), (0, 2), (1, 2))


def one_axis_at_a_time(array, axes):
    return functools.reduce(lax.psum, axes, array)


def cut_along(array, dim, count):
    before, after = (array.shape[:dim], array.shape[dim + 1 :])
    return jnp.moveaxis(array.reshape(*before, count, -1, *after), dim, 0)


def piece_ends(length, count):
    unit = 8 if length >= 8 * count else 1
    return [length // unit * k // count * unit for k in range(1, count)]


def in_order(tiles, dim):
    tiles = jnp.moveaxis(tiles, 0, dim)
    lengths = tiles.shape
    return tiles.reshape(*lengths[:dim], lengths[dim] * lengths[dim + 1], *lengths[dim + 2 :])


def cut_exchange(array, axis, pieces, split_dim, concat_dim):
    tiles = cut_along(array, split_dim, lax.axis_size(axis))
    cut = max(range(1, max(2, tiles.ndim - 1)), key=lambda d: tiles.shape[d])
    done = []
    for section in jnp.split(tiles, piece_ends(tiles.shape[cut], pieces), axis=cut):
        if section.size:
            done.append(lax.all_to_all(section, axis, split_axis=0, concat_axis=0, tiled=True))
    return in_order(jnp.concatenate(done, axis=cut), concat_dim)


def dft_tables(length):
    counter = jnp.arange(length, dtype=jnp.int32)
    phases = counter[:, None] * counter[None, :] % length
    angles = phases.astype(jnp.float32) * (2.0 * math.pi / length)
    return (jnp.cos(angles).astype(jnp.bfloat16), jnp.sin(angles).astype(jnp.bfloat16))


def twiddle(rows, cols):
    phases = jnp.arange(rows, dtype=jnp.int32)[:, None] * jnp.arange(cols, dtype=jnp.int32)[None, :]
    angles = phases.astype(jnp.float32) * (2.0 * math.pi / (rows * cols))
    return (jnp.cos(angles), jnp.sin(angles))


def mult(table, data, form):
    return jnp.einsum(form, table, data, preferred_element_type=jnp.float32)


def spectra(strain, rows, cols):
    lead = strain.shape[:3]
    real_in = strain[:, :, :, 0].reshape(-1, rows, cols)
    imag_in = strain[:, :, :, 1].reshape(-1, rows, cols)
    cos_rows, sin_rows = dft_tables(rows)
    first_real = mult(cos_rows, real_in, "kn,bnq->bkq") + mult(sin_rows, imag_in, "kn,bnq->bkq")
    first_imag = mult(cos_rows, imag_in, "kn,bnq->bkq") - mult(sin_rows, real_in, "kn,bnq->bkq")
    tw_cos, tw_sin = twiddle(rows, cols)
    mid_real = (first_real * tw_cos + first_imag * tw_sin).astype(jnp.bfloat16)
    mid_imag = (first_imag * tw_cos - first_real * tw_sin).astype(jnp.bfloat16)
    cos_cols, sin_cols = dft_tables(cols)
    last_real = mult(cos_cols, mid_real, "kn,bpn->bkp") + mult(sin_cols, mid_imag, "kn,bpn->bkp")
    last_imag = mult(cos_cols, mid_imag, "kn,bpn->bkp") - mult(sin_cols, mid_real, "kn,bpn->bkp")
    scale = 1.0 / math.sqrt(rows * cols)
    shape = lead + (rows * cols,)
    return (last_real.reshape(shape) * scale, last_imag.reshape(shape) * scale)


def segment_stats(real_part, imag_part, valid_float):
    power = jnp.mean(real_part * real_part + imag_part * imag_part, axis=2)
    weights = []
    weighted = []
    for first, second in baseline_pairs:
        cross = jnp.mean(
            real_part[first] * real_part[second] + imag_part[first] * imag_part[second], axis=1
        )
        weight = valid_float[:, None] / (power[first] * power[second])
        weights.append(weight)
        weighted.append(weight * cross)
    return jnp.stack(weights + weighted, axis=1)


def local(strain, valid, intersection, notch):
    total_bins = intersection.shape[1]
    devices = lax.axis_size(SEG)
    local_bins = total_bins // devices
    rows = FA
    cols = FB
    real_part, imag_part = spectra(strain, rows, cols)
    stats = segment_stats(real_part, imag_part, valid.astype(jnp.float32))
    kept_all = notch.astype(jnp.float32)[None, :]
    own_weights = jnp.sum(stats[:, :3], axis=0)
    own_numer = jnp.sum(stats[:, 3:], axis=0)
    signal, info = (
        one_axis_at_a_time(jnp.sum(kept_all * intersection * own_numer, axis=1), SEG),
        one_axis_at_a_time(
            jnp.sum(kept_all * intersection * intersection * own_weights, axis=1), SEG
        ),
    )
    moved = cut_exchange(stats, SEG, 2, 2, 0)
    sums = jnp.sum(moved, axis=0)
    start = lax.axis_index(SEG) * local_bins
    intersection_local = lax.dynamic_slice_in_dim(intersection, start, local_bins, 1)
    kept = lax.dynamic_slice_in_dim(notch, start, local_bins, 0).astype(jnp.float32)[None, :]
    numer = sums[3:]
    contribution = kept * intersection_local * numer / jnp.sqrt(info / total_bins)[:, None]
    broadband = jnp.stack([signal / jnp.sqrt(info), jnp.sqrt(info / total_bins)], axis=1)
    return (contribution, broadband)


def solution(mesh):
    split = Mesh(mesh.devices.reshape(4, 4, 4, 2), ("seg_0", "seg_1", "seg_2", "seg_3"))
    in_specs = (P(None, SEG, None, None, None), P(SEG), P(), P())
    out_specs = (P(None, SEG), P())
    return jax.shard_map(local, mesh=split, in_specs=in_specs, out_specs=out_specs, check_vma=False)
```

profile of v0, /device:TPU:1, one launch (start us, length us, event | category | flops | bytes accessed | tf_op | source)
XLA Modules:
  0.0 205.3 jit_solution(9227705165203348343)
XLA Ops:
  1.6 26.4 %slice_reduce_fusion = (bf16[3,2,3,65536]{3,2,1,0:T(4,128)(2,1)}, bf16[3,2,3,65536]{3,2,1,0:T(4,128)(2,1)}) fusion(bf16[3,2,3,2,65536]{4,3,2,1,0:T(2,128)(2,1)} %param.4), kind=kLoop, calls=%fused_computation.5 | loop fusion | bytes 9437184 | tf_op jit(solution)/shard_map/slice | solution.py:68
  28.0 5.4 %reshape_squeeze.7 = bf16[18,256,256]{2,1,0:T(8,128)(2,1)S(1)} reshape(bf16[3,2,3,65536]{3,2,1,0:T(4,128)(2,1)} %get-tuple-element.2) | data formatting | bytes 4718592 | tf_op jit(solution)/shard_map/reshape;squeeze | solution.py:68
  33.4 3.8 %fusion.26 = f32[256,18,256]{2,0,1:T(8,128)} fusion(bf16[18,256,256]{2,1,0:T(8,128)(2,1)S(1)} %reshape_squeeze.7), kind=kOutput, calls=%fused_computation.63 | convolution fusion | flops 604962816 | bytes 7077888 | tf_op jit(solution)/shard_map/kn,bnq->bkq/dot_general | solution.py:62
  37.2 6.5 %reshape_squeeze.6 = bf16[18,256,256]{2,1,0:T(8,128)(2,1)} reshape(bf16[3,2,3,65536]{3,2,1,0:T(4,128)(2,1)} %get-tuple-element.3) | data formatting | bytes 4718592 | tf_op jit(solution)/shard_map/reshape;squeeze | solution.py:67
  43.7 3.5 %fusion.28 = f32[256,18,256]{2,0,1:T(8,128)S(1)} fusion(bf16[18,256,256]{2,1,0:T(8,128)(2,1)} %reshape_squeeze.6), kind=kOutput, calls=%fused_computation.64 | convolution fusion | flops 604962816 | bytes 7077888 | tf_op jit(solution)/shard_map/kn,bnq->bkq/dot_general | solution.py:62
  49.1 3.5 %fusion = (bf16[18,256,256]{2,1,0:T(8,128)(2,1)S(1)}, bf16[18,256,256]{2,1,0:T(8,128)(2,1)S(1)}) fusion(f32[256,18,256]{2,0,1:T(8,128)S(1)} %convolution_subtract_fusion, f32[256,256]{1,0:T(8,128)S(1)} %get-tuple-element.41, f32[256,256]{1,0:T(8,128)S(1)} %get-tuple-element.42, f32[256,18,256]{2,0,1:T(8,128)S(1)} %fusion.28, ...), kind=kOutput, calls=%fused_computation.8 | convolution fusion | flops 615579648 | bytes 17039360 | tf_op jit(solution)/shard_map/kn,bnq->bkq/dot_general | solution.py:62
  57.8 4.3 %multiply_add_fusion = (f32[18,256,256]{1,2,0:T(8,128)}, f32[18,256,256]{1,2,0:T(8,128)S(1)}) fusion(f32[18,256,256]{1,2,0:T(8,128)S(1)} %multiply_bitcast_fusion.1, f32[18,256,256]{2,1,0:T(8,128)S(1)} %fusion.22, bf16[18,256,256]{2,1,0:T(8,128)(2,1)S(1)} %get-tuple-element.23), kind=kOutput, calls=%fused_computation | convolution fusion | flops 610861056 | bytes 21233664 | tf_op jit(solution)/shard_map/kn,bpn->bkp/dot_general | solution.py:62
  68.2 3.1 %copy.22 = f32[6,256,256]{2,1,0:T(8,128)} copy(f32[6,256,256]{1,2,0:T(8,128)} %get-tuple-element.26) | data formatting | bytes 3145728 | tf_op jit(solution)/shard_map/add | solution.py:89
  71.3 3.0 %add.103 = f32[2,3,65536]{2,1,0:T(4,128)} reshape(f32[6,256,256]{2,1,0:T(8,128)} %copy.22) | data formatting | bytes 3145728 | tf_op jit(solution)/shard_map/add | solution.py:89
  75.9 3.2 %reduce_sum.83 = f32[2,65536]{1,0:T(2,128)S(1)} reduce(f32[2,3,65536]{2,1,0:T(4,128)} %add.103, f32[]{:T(128)} %constant.59.clone.1), dimensions={1}, to_apply=%region_2.3 | reduce | flops 262144 | bytes 2097156 | tf_op jit(solution)/shard_map/reduce_sum | solution.py:88
  82.9 2.4 %reduce_sum.84 = f32[2,65536]{1,0:T(2,128)} reduce(f32[2,3,65536]{2,1,0:T(4,128)S(1)} %add.105, f32[]{:T(128)} %constant.59.clone.1), dimensions={1}, to_apply=%region_3.4 | reduce | flops 262144 | bytes 2097156 | tf_op jit(solution)/shard_map/reduce_sum | solution.py:88
  85.3 6.1 %copy.20 = f32[18,256,256]{2,1,0:T(8,128)} copy(f32[18,256,256]{1,2,0:T(8,128)} %get-tuple-element.39) | data formatting | bytes 9437184 | tf_op jit(solution)/shard_map/add | solution.py:84
  91.4 7.5 %add.99 = f32[3,2,3,65536]{3,2,1,0:T(4,128)} reshape(f32[18,256,256]{2,1,0:T(8,128)} %copy.20) | data formatting | bytes 9437184 | tf_op jit(solution)/shard_map/add | solution.py:84
  98.9 7.4 %reduce_sum.81 = f32[3,2,65536]{2,1,0:T(2,128)S(1)} reduce(f32[3,2,3,65536]{3,2,1,0:T(4,128)} %add.99, f32[]{:T(128)} %constant.59.clone.1), dimensions={2}, to_apply=%region_0.1 | reduce | flops 786432 | bytes 6291460 | tf_op jit(solution)/shard_map/reduce_sum | solution.py:84
  107.9 2.9 %bitcast_multiply_fusion.3 = (f32[2,1,65536]{2,0,1:T(2,128)}, f32[2,1,65536]{2,0,1:T(2,128)}, f32[1,2,65536]{2,1,0:T(2,128)S(1)}, f32[2,1,65536]{2,0,1:T(2,128)}...) fusion(f32[2,65536]{1,0:T(2,128)S(1)} %copy-done.3, ...), kind=kLoop, calls=%fused_computation.32 | loop fusion | flops 1572864 | bytes 7864328 | tf_op jit(solution)/shard_map/mul | solution.py:93
  114.7 11.8 %all-to-all-start = ((f32[128,2,3,512]{3,1,2,0:T(2,128)}), f32[128,2,3,512]{3,1,2,0:T(2,128)S(1)}, u32[]{:S(2)}, u32[]{:S(2)}) async-start(f32[128,2,3,512]{3,1,2,0:T(2,128)} %copy.24), calls=%async_computation | async-start | bytes 3145728 | tf_op jit(solution)/shard_map/all_to_all | solution.py:44
  126.5 2.4 %copy.25 = f32[128,2,3,512]{3,1,2,0:T(2,128)} copy(f32[128,2,3,512]{3,0,1,2:T(8,128)S(1)} %get-tuple-element.29) | data formatting | bytes 3145728 | tf_op jit(solution)/shard_map/split | solution.py:42
  128.9 22.1 %all-to-all-done = f32[128,2,3,512]{3,1,2,0:T(2,128)S(1)} async-done(((f32[128,2,3,512]{3,1,2,0:T(2,128)}), f32[128,2,3,512]{3,1,2,0:T(2,128)S(1)}, u32[]{:S(2)}, u32[]{:S(2)}) %all-to-all-start) | async-done | bytes 1572896 | tf_op jit(solution)/shard_map/all_to_all | solution.py:44
  151.0 4.8 %all-to-all-start.1 = ((f32[128,2,3,512]{3,1,2,0:T(2,128)}), f32[128,2,3,512]{3,1,2,0:T(2,128)S(1)}, u32[]{:S(2)}, u32[]{:S(2)}) async-start(f32[128,2,3,512]{3,1,2,0:T(2,128)} %copy.25), calls=%async_computation.1 | async-start | bytes 3145728 | tf_op jit(solution)/shard_map/all_to_all | solution.py:44
  155.8 3.9 %maximum_reduce_fusion.1 = f32[3,65536]{1,0:T(4,128)S(1)} fusion(f32[2,1,65536]{2,0,1:T(2,128)} %get-tuple-element.21, f32[2,1,65536]{2,0,1:T(2,128)} %get-tuple-element.31, f32[2,1,65536]{2,0,1:T(2,128)} %get-tuple-element.34), kind=kLoop, calls=%fused_computation.12 | loop fusion | flops 983040 | bytes 2359296 | tf_op jit(solution)/shard_map/reduce_sum | solution.py:106
  163.0 11.1 %all-reduce.2 = (f32[3]{0:T(128)S(1)}, f32[3]{0:T(128)S(1)}) all-reduce(f32[3]{0:T(128)S(1)} %get-tuple-element.5, f32[3]{0:T(128)S(1)} %get-tuple-element.4), channel_id=1, replica_groups=mesh['seg_0'=4,'seg_1'=4,'seg_2'=4,'seg_3'=2] {'seg_0'}, use_global_device_ids=true, to_apply=%region_7.8 | all-reduce | flops 6 | bytes 48 | tf_op jit(solution)/shard_map/psum | solution.py:19
  174.1 10.9 %all-reduce.1 = (f32[3]{0:T(128)S(1)}, f32[3]{0:T(128)S(1)}) all-reduce(f32[3]{0:T(128)S(1)} %get-tuple-element.10, f32[3]{0:T(128)S(1)} %get-tuple-element.11), channel_id=1, replica_groups=mesh['seg_0'=4,'seg_1'=4,'seg_2'=4,'seg_3'=2] {'seg_1'}, use_global_device_ids=true, to_apply=%region_8.9 | all-reduce | flops 6 | bytes 48 | tf_op jit(solution)/shard_map/psum | solution.py:19
  184.9 9.2 %all-reduce = (f32[3]{0:T(128)S(1)}, f32[3]{0:T(128)S(1)}) all-reduce(f32[3]{0:T(128)S(1)} %get-tuple-element.8, f32[3]{0:T(128)S(1)} %get-tuple-element.9), channel_id=1, replica_groups=mesh['seg_0'=4,'seg_1'=4,'seg_2'=4,'seg_3'=2] {'seg_2'}, use_global_device_ids=true, to_apply=%region_9.10 | all-reduce | flops 6 | bytes 48 | tf_op jit(solution)/shard_map/psum | solution.py:19
  194.1 7.6 %all-reduce.3 = (f32[3]{0:T(128)S(1)}, f32[3]{0:T(128)S(1)}) all-reduce(f32[3]{0:T(128)S(1)} %get-tuple-element.6, f32[3]{0:T(128)S(1)} %get-tuple-element.7), channel_id=1, replica_groups=mesh['seg_0'=4,'seg_1'=4,'seg_2'=4,'seg_3'=2] {'seg_3'}, use_global_device_ids=true, to_apply=%region_10.11 | all-reduce | flops 6 | bytes 48 | tf_op jit(solution)/shard_map/psum | solution.py:19
  (53 shorter events, 31.3 us)
Async XLA Ops:
  43.7 3.5 %copy-start = (bf16[18,256,256]{2,1,0:T(8,128)(2,1)S(1)}, bf16[18,256,256]{2,1,0:T(8,128)(2,1)}, u32[]{:S(2)}) copy-start(bf16[18,256,256]{2,1,0:T(8,128)(2,1)} %reshape_squeeze.6) | copy-start | bytes 7077892
  43.7 3.8 %copy-start.1 = (f32[256,18,256]{2,0,1:T(8,128)S(1)}, f32[256,18,256]{2,0,1:T(8,128)}, u32[]{:S(2)}) copy-start(f32[256,18,256]{2,0,1:T(8,128)} %fusion.26) | copy-start | bytes 14155780
  75.9 3.2 %copy-start.2 = (f32[6,256,256]{1,2,0:T(8,128)S(1)}, f32[6,256,256]{1,2,0:T(8,128)}, u32[]{:S(2)}) copy-start(f32[6,256,256]{1,2,0:T(8,128)} %get-tuple-element.25) | copy-start | bytes 4718596
  106.2 0.8 copy-start.9
  106.2 1.4 copy-start.3
  114.7 36.3 %all-to-all-start = ((f32[128,2,3,512]{3,1,2,0:T(2,128)}), f32[128,2,3,512]{3,1,2,0:T(2,128)S(1)}, u32[]{:S(2)}, u32[]{:S(2)}) async-start(f32[128,2,3,512]{3,1,2,0:T(2,128)} %copy.24), calls=%async_computation | async-start | bytes 3145728 | tf_op jit(solution)/shard_map/all_to_all | solution.py:44
  128.9 26.9 %copy-start.8 = (s32[65536]{0:T(1024)S(1)}, s32[65536]{0:T(1024)}, u32[]{:S(2)}) copy-start(s32[65536]{0:T(1024)} %param.7) | copy-start | bytes 786436
  151.0 51.4 %all-to-all-start.1 = ((f32[128,2,3,512]{3,1,2,0:T(2,128)}), f32[128,2,3,512]{3,1,2,0:T(2,128)S(1)}, u32[]{:S(2)}, u32[]{:S(2)}) async-start(f32[128,2,3,512]{3,1,2,0:T(2,128)} %copy.25), calls=%async_computation.1 | async-start | bytes 3145728 | tf_op jit(solution)/shard_map/all_to_all | solution.py:44
  155.8 4.0 %copy-start.4 = (f32[2,1,65536]{2,0,1:T(2,128)S(1)}, f32[2,1,65536]{2,0,1:T(2,128)}, u32[]{:S(2)}) copy-start(f32[2,1,65536]{2,0,1:T(2,128)} %get-tuple-element.20) | copy-start | bytes 1572868
  155.8 4.0 %copy-start.5 = (f32[2,1,65536]{2,0,1:T(2,128)S(1)}, f32[2,1,65536]{2,0,1:T(2,128)}, u32[]{:S(2)}) copy-start(f32[2,1,65536]{2,0,1:T(2,128)} %get-tuple-element.30) | copy-start | bytes 1572868
  155.8 4.0 %copy-start.6 = (f32[2,1,65536]{2,0,1:T(2,128)S(1)}, f32[2,1,65536]{2,0,1:T(2,128)}, u32[]{:S(2)}) copy-start(f32[2,1,65536]{2,0,1:T(2,128)} %get-tuple-element.33) | copy-start | bytes 1572868
  155.8 6.3 %copy-start.7 = (f32[3,65536]{1,0:T(4,128)S(1)}, f32[3,65536]{1,0:T(4,128)}, u32[]{:S(2)}) copy-start(f32[3,65536]{1,0:T(4,128)} %param.6) | copy-start | bytes 2359300
where the time goes:
time: 209 us; the launch traced here: 205 us
  local copies, waits for them, and re-layouts  70.7 us (34%)
  blocking collectives  38.7 us (19%)
  other arithmetic  34 us (16%)
  waiting for transfers between devices  22.1 us (11%)
  matrix products  21.9 us (10%)
  starting transfers between devices  16.6 us (8%)
    psum x4, blocking collectives, one_axis_at_a_time(): return functools.reduce(lax.psum, axes, array)  38.7 us
    slice x1, local copies, waits for them, and re-layouts, spectra(): imag_in = strain[:, :, :, 1].reshape(-1, rows, cols)  26.4 us
    all_to_all x2, waiting for transfers between devices, cut_exchange(): lax.all_to_all(section, axis, split_axis=0, concat_axis=0, tiled=True)  22.1 us
    dot_general x8, matrix products, mult(): return jnp.einsum(form, table, data, preferred_element_type=jnp.float32)  21.9 us
    all_to_all x2, starting transfers between devices, cut_exchange(): lax.all_to_all(section, axis, split_axis=0, concat_axis=0, tiled=True)  16.6 us
    add x2, local copies, waits for them, and re-layouts, segment_stats(): power = jnp.mean(real_part * real_part + imag_part * imag_part, axis=2)  13.6 us
    add x6, local copies, waits for them, and re-layouts, segment_stats(): real_part[first] * real_part[second] + imag_part[first] * imag_part[second]  13.5 us
    reduce_sum x1, other arithmetic, segment_stats(): power = jnp.mean(real_part * real_part + imag_part * imag_part, axis=2)  7.37 us
  transfers between devices with their start and end apart: 2, of which 1 were waited for; matrix products, arithmetic and copies ran while one was open for 5% of the time, Pallas kernels for 0%

commit v1 on v0

v1 whole, which is shorter than its diff:
```python
import functools
import math

import jax
import jax.numpy as jnp
import numpy as np
from jax import lax
from jax.experimental import pallas as pl
from jax.experimental.pallas import tpu as pltpu
from jax.sharding import PartitionSpec as P

MESH = pl.DeviceIdType.MESH
F = 256
BINS = F * F
CHIPS = 64
PAIRS = ((0, 1), (0, 2), (1, 2))
ROWS = 64
f32, bf16 = jnp.float32, jnp.bfloat16


def tables():
    k = np.arange(F)
    angle = 2 * np.pi * ((k[:, None] * k[None, :]) % F) / F
    cos, sin = (t(angle).astype(bf16).astype(np.float32) for t in (np.cos, np.sin))
    s = np.arange(8)
    a_of = (8 * np.arange(32)[:, None] + (s // 2 + 4 * (s % 2))[None, :]).reshape(-1)
    one = np.zeros((2, F, F, 2), np.float32)
    one[0, :, :, 0], one[0, :, :, 1] = cos[:, a_of], sin[:, a_of]
    one[1, :, :, 0], one[1, :, :, 1] = -sin[:, a_of], cos[:, a_of]
    one = one.reshape(2, 16, 16, 512).transpose(1, 0, 2, 3).reshape(512, 512)
    one = one.reshape(512, 4, 128).transpose(1, 0, 2)
    w, r, chip = np.meshgrid(np.arange(2), np.arange(2), np.arange(CHIPS), indexing="ij")
    q_of = (4 * chip + 2 * w + r).reshape(-1)
    c, v = cos[:, q_of] / F, sin[:, q_of] / F
    two = np.block([[c, -v], [v, c]])
    two = two.reshape(512, 4, 128).transpose(1, 0, 2)
    turn = 2 * np.pi * (k[:, None] * k[None, :]) / BINS
    turns = np.stack([np.cos(turn), np.sin(turn)]).astype(np.float32)
    return one.astype(bf16), two.astype(bf16), turns


def kernel(valid, strain, inter, notch, one, two, turns, out, board,
           x, l1, l2, uv, it, nt, at, mid, y, part, num, came, send, recv, sc, sccame,
           load_sem, x_sem, pair_sem, out_sem, in_sem):
    me = lax.axis_index("seg")
    chip, core = me // 2, lax.rem(me, 2)
    mate = me + 1 - 2 * core

    loads = [pltpu.make_async_copy(a, b, load_sem.at[n]) for n, (a, b) in enumerate(
        ((inter, it.at[:, :3]), (notch, nt), (one, l1), (turns, uv), (two, l2)))]
    takes = [pltpu.make_async_copy(strain.at[n], x.at[n], x_sem.at[n]) for n in range(18)]
    for c in loads[:4] + takes + loads[4:]:
        c.start()

    barrier = pltpu.get_barrier_semaphore()
    pl.semaphore_signal(barrier, inc=1, device_id=(mate,), device_id_type=MESH)

    @pl.loop(1, CHIPS)
    def _(r):
        to = lax.rem(chip + r, CHIPS) * 2 + core
        pl.semaphore_signal(barrier, inc=1, device_id=(to,), device_id_type=MESH)

    loads[0].wait()
    loads[1].wait()
    rows4 = it.reshape(2048, 128)
    for h in range(2):
        for w in range(2):
            keep = [nt[pl.ds(2 * (2 * w + r) + h, CHIPS, stride=8), :].astype(f32) for r in range(2)]
            for i in range(3):
                got = [rows4[pl.ds(8 * (2 * w + r) + 4 * h + i, CHIPS, stride=32), :] * keep[r] for r in range(2)]
                at[i, h, :, w * 128:(w + 1) * 128] = jnp.concatenate(got, axis=0).T

    even = (lax.broadcasted_iota(jnp.int16, (16, 128), 0) & 2) == 0
    loads[2].wait()
    loads[3].wait()
    for n in range(18):
        takes[n].wait()
        left, right = [], []
        for g in range(32):
            a, b = x[n, pl.ds(32 * g, 16), :], x[n, pl.ds(32 * g + 16, 16), :]
            left.append(jnp.where(even, a, pltpu.roll(b, 2, axis=0)))
            right.append(jnp.where(even, pltpu.roll(a, 14, axis=0), b))
        data = jnp.concatenate([jnp.concatenate(left, 0), jnp.concatenate(right, 0)], axis=1)
        table = jnp.concatenate([l1[k] for k in range(4)], axis=1)
        first = jnp.dot(table, data, preferred_element_type=f32)
        for g in range(16):
            re, im = first[32 * g:32 * g + 16], first[32 * g + 16:32 * g + 32]
            u, v = uv[0, pl.ds(16 * g, 16), :], uv[1, pl.ds(16 * g, 16), :]
            mr = (re * u + im * v).astype(bf16)
            mi = (im * u - re * v).astype(bf16)
            for h in range(2):
                mid[n, h, pl.ds(16 * g, 16), :] = mr[:, 128 * h:128 * h + 128]
                mid[n, 2 + h, pl.ds(16 * g, 16), :] = mi[:, 128 * h:128 * h + 128]

    loads[4].wait()
    pl.semaphore_wait(barrier, CHIPS)

    def second(block, s, slot):
        rows = pl.ds(ROWS * block, ROWS)
        which = [d * 6 + s * 3 + t for t in range(3) for d in range(3)]
        data = jnp.concatenate(
            [jnp.concatenate([mid[n, k, rows, :] for n in which], axis=0) for k in range(4)], axis=1)
        table = jnp.concatenate([l2[k] for k in range(4)], axis=1)
        y[slot] = jnp.dot(data, table, preferred_element_type=f32)

    signal = [jnp.zeros((8, 128), f32)] * 3
    info = [jnp.zeros((8, 128), f32)] * 3

    def stats(block, s, slot):
        ok = valid[s].astype(f32)
        for g in range(ROWS // 8):
            for w in range(2):
                lane = slice(128 * w, 128 * w + 128)
                lane_im = slice(256 + 128 * w, 384 + 128 * w)
                power = [None] * 3
                cross = [None] * 3
                for t in range(3):
                    at_row = lambda d: pl.ds(ROWS * (3 * t + d) + 8 * g, 8)
                    re = [y[slot, at_row(d), lane] for d in range(3)]
                    im = [y[slot, at_row(d), lane_im] for d in range(3)]
                    for d in range(3):
                        v = re[d] * re[d] + im[d] * im[d]
                        power[d] = v if t == 0 else power[d] + v
                    for i, (a, b) in enumerate(PAIRS):
                        v = re[a] * re[b] + im[a] * im[b]
                        cross[i] = v if t == 0 else cross[i] + v
                third = [p * (1.0 / 3.0) for p in power]
                half, row = divmod(ROWS * block + 8 * g, 128)
                row = pl.ds(row, 8)
                for i, (a, b) in enumerate(PAIRS):
                    weight = ok / (third[a] * third[b])
                    v = weight * (cross[i] * (1.0 / 3.0))
                    f = at[i, half, row, lane]
                    signal[i] = signal[i] + f * v
                    info[i] = info[i] + f * f * weight
                    if s == 0:
                        part[i, half, row, lane] = v
                    else:
                        part[i, half, row, lane] = part[i, half, row, lane] + v

    def pair(half):
        return pltpu.make_async_remote_copy(
            src_ref=num.at[half, 1 - core], dst_ref=came.at[half],
            send_sem=pair_sem.at[half], recv_sem=pair_sem.at[2 + half],
            device_id=(mate,), device_id_type=MESH)

    def turn(half):
        for w in range(2):
            for i in range(3):
                num[half, w, i] = part[i, half, :, w * 128:(w + 1) * 128].T

    def merge(half):
        for i in range(3):
            for r in range(2):
                send[half, pl.ds(2 * i + r, CHIPS, stride=8), :] = (
                    num[half, core, i, pl.ds(CHIPS * r, CHIPS), :] + came[half, i, pl.ds(CHIPS * r, CHIPS), :])

    def spread(half):
        @pl.loop(1, CHIPS)
        def _(r):
            to = lax.rem(chip + r, CHIPS)
            pltpu.make_async_remote_copy(
                src_ref=send.at[half, pl.ds(pl.multiple_of(8 * to, 8), 8)],
                dst_ref=recv.at[half, pl.ds(pl.multiple_of(8 * (r - 1), 8), 8)],
                send_sem=out_sem.at[half], recv_sem=in_sem.at[half],
                device_id=(2 * to + core,), device_id_type=MESH).start()

    order = [(block, s) for block in range(F // ROWS) for s in range(2)]
    for n, (block, s) in enumerate(order):
        second(block, s, n % 2)
        if n:
            stats(*order[n - 1], (n - 1) % 2)
        if n == 5:
            turn(0)
            pair(0).start()
    stats(*order[-1], 1)
    turn(1)
    rows = [jnp.sum(a, axis=0, keepdims=True) for a in signal + info]
    cells = [jnp.sum(a, axis=1, keepdims=True) for a in rows]
    lanes = lax.broadcasted_iota(jnp.int32, (1, 128), 1)
    lines = []
    for group in (cells[:3], cells[3:]):
        line = jnp.zeros((1, 128), f32)
        for i in range(3):
            line = jnp.where(lanes == i, group[i], line)
        lines.append(line)
    sc[...] = jnp.concatenate(lines + [jnp.zeros((6, 128), f32)], axis=0)
    scalars = pltpu.make_async_remote_copy(
        src_ref=sc, dst_ref=sccame, send_sem=pair_sem.at[4], recv_sem=pair_sem.at[5],
        device_id=(mate,), device_id_type=MESH)
    pair(1).start()
    scalars.start()
    pair(0).wait()
    for r in range(2):
        send[0, pl.ds(6 + r, CHIPS, stride=8), :] = jnp.zeros((CHIPS, 128), f32)
    merge(0)
    spread(0)
    pair(1).wait()
    scalars.wait()
    both = sc[...] + sccame[...]
    for r in range(2):
        send[1, pl.ds(6 + r, CHIPS, stride=8), :] = jnp.broadcast_to(both[r:r + 1], (CHIPS, 128))
    merge(1)
    spread(1)

    totals = []
    for half in range(2):
        whole = recv.at[half]
        pltpu.make_async_copy(whole, whole, in_sem.at[half]).wait()
        total = send[half, pl.ds(pl.multiple_of(8 * chip, 8), 8), :]
        for r in range(CHIPS - 1):
            total = total + recv[half, pl.ds(8 * r, 8), :]
        totals.append(total)
    for half in range(2):
        whole = recv.at[half]
        pltpu.make_async_copy(whole, whole, out_sem.at[half]).wait()
    own = it[pl.ds(4 * me, 4)]
    kept = nt[pl.ds(4 * me, 4), :].astype(f32)
    for i in range(3):
        sig = totals[1][6:7, i:i + 1]
        inf = totals[1][7:8, i:i + 1]
        root = jnp.sqrt(inf * (1.0 / BINS))
        for r in range(2):
            for h in range(2):
                t = 2 * r + h
                row = totals[h][2 * i + r:2 * i + r + 1]
                out[t, i:i + 1] = kept[t:t + 1] * own[t, i:i + 1] * row / root
        board[i:i + 1, 0:1] = sig / jnp.sqrt(inf)
        board[i:i + 1, 1:2] = root


def local(strain, valid, intersection, notch):
    one, two, turns = tables()
    strain = strain.reshape(18, 2, 512, 128).transpose(0, 2, 1, 3).reshape(18, 1024, 128)
    inter = intersection.reshape(3, 512, 128).transpose(1, 0, 2)
    out, board = pl.pallas_call(
        kernel,
        out_shape=(jax.ShapeDtypeStruct((4, 3, 128), f32), jax.ShapeDtypeStruct((3, 2), f32)),
        in_specs=[pl.BlockSpec(memory_space=pltpu.SMEM)] + [pl.BlockSpec(memory_space=pl.ANY)] * 6,
        out_specs=(pl.BlockSpec(memory_space=pltpu.VMEM), pl.BlockSpec(memory_space=pltpu.VMEM)),
        scratch_shapes=[
            pltpu.VMEM((18, 1024, 128), bf16),
            pltpu.VMEM((4, 512, 128), bf16),
            pltpu.VMEM((4, 512, 128), bf16),
            pltpu.VMEM((2, F, F), f32),
            pltpu.VMEM((512, 4, 128), f32),
            pltpu.VMEM((512, 128), jnp.int32),
            pltpu.VMEM((3, 2, 128, F), f32),
            pltpu.VMEM((18, 4, F, 128), bf16),
            pltpu.VMEM((2, 9 * ROWS, 512), f32),
            pltpu.VMEM((3, 2, 128, F), f32),
            pltpu.VMEM((2, 2, 3, 128, 128), f32),
            pltpu.VMEM((2, 3, 128, 128), f32),
            pltpu.VMEM((2, 8 * CHIPS, 128), f32),
            pltpu.VMEM((2, 8 * (CHIPS - 1), 128), f32),
            pltpu.VMEM((8, 128), f32),
            pltpu.VMEM((8, 128), f32),
            pltpu.SemaphoreType.DMA((5,)),
            pltpu.SemaphoreType.DMA((18,)),
            pltpu.SemaphoreType.DMA((6,)),
            pltpu.SemaphoreType.DMA((2,)),
            pltpu.SemaphoreType.DMA((2,)),
        ],
        compiler_params=pltpu.CompilerParams(
            collective_id=0, has_side_effects=True, vmem_limit_bytes=60 * 2**20),
    )(valid, strain, inter, notch.reshape(512, 128), jnp.asarray(one), jnp.asarray(two), jnp.asarray(turns))
    return out.transpose(1, 0, 2).reshape(3, 512), board


def solution(mesh):
    in_specs = (P(None, "seg", None, None, None), P("seg"), P(), P())
    return jax.shard_map(local, mesh=mesh, in_specs=in_specs, out_specs=(P(None, "seg"), P()), check_vma=False)
```

time: 209 us -> 33.6 us (0.16); the launches traced: 205 us -> 33.3 us
  local copies, waits for them, and re-layouts: 70.7 us -> 2.59 us
  blocking collectives: 38.7 us -> 0 us
  other arithmetic: 34 us -> 0 us
  Pallas kernels: 0 us -> 30.1 us
  waiting for transfers between devices: 22.1 us -> 0 us
  matrix products: 21.9 us -> 0 us
  starting transfers between devices: 16.6 us -> 0 us
    psum x4 -> x0, blocking collectives: 38.7 us -> none  [one_axis_at_a_time(): return functools.reduce(lax.psum, axes, array)]
    pallas_call x0 -> x1, Pallas kernels: none -> 30.1 us  [local(): pl.pallas_call(kernel, out_shape=(jax.ShapeDtypeStruct((4, 3, 128), f32),...]
    add x8 -> x0, local copies, waits for them, and re-layouts: 27.1 us -> none  [the longest x2 13.6 us: segment_stats(): power = jnp.mean(real_part * real_part + imag_part * imag_part, axis=2)]
    slice x1 -> x0, local copies, waits for them, and re-layouts: 26.4 us -> none  [spectra(): imag_in = strain[:, :, :, 1].reshape(-1, rows, cols)]
    reduce_sum x8 -> x0, other arithmetic: 23 us -> none  [the longest x1 7.37 us: segment_stats(): power = jnp.mean(real_part * real_part + imag_part * imag_part, axis=2)]
    all_to_all x2 -> x0, waiting for transfers between devices: 22.1 us -> none  [cut_exchange(): lax.all_to_all(section, axis, split_axis=0, concat_axis=0, tiled=True)]
    dot_general x8 -> x0, matrix products: 21.9 us -> none  [mult(): return jnp.einsum(form, table, data, preferred_element_type=jnp.float32)]
    all_to_all x2 -> x0, starting transfers between devices: 16.6 us -> none  [cut_exchange(): lax.all_to_all(section, axis, split_axis=0, concat_axis=0, tiled=True)]
  transfers between devices with their start and end apart: 2 -> 0, of which waited for: 1 -> 0; matrix products, arithmetic and copies ran while one was open for 5% -> 0% of each run, Pallas kernels for 0% -> 0%
where the time goes in v1:
time: 33.6 us; the launch traced here: 33.3 us
  Pallas kernels  30.1 us (90%)
  local copies, waits for them, and re-layouts  2.59 us (8%)
  between operations  0.64 us (2%)
    pallas_call x1, Pallas kernels, local(): pl.pallas_call(kernel, out_shape=(jax.ShapeDtypeStruct((4, 3, 128), f32),...  30.1 us
    unnamed x2, local copies, waits for them, and re-layouts  2.59 us

profile of v1, /device:TPU:1, one launch (start us, length us, event | category | flops | bytes accessed | tf_op | source)
XLA Modules:
  0.0 33.3 jit_solution(13964091105652036004)
XLA Ops:
  0.6 30.1 %shard_map.86 = (f32[4,3,128]{2,1,0:T(4,128)}, f32[3,2]{1,0:T(4,128)}) custom-call(s32[2]{0:T(128)} %valid.1, bf16[18,1024,128]{2,1,0:T(8,128)(2,1)} %bitcast.12, f32[512,3,128]{2,1,0:T(4,128)} %bitcast.13, s32[512,128]{1,0:T(8,128)} %bitcast.14, bf16[4,512,128]{2,1,0:T(8,128)(2,1)} %constant.6.clone.one, bf16[4,512,128]{2,1,0:T(8,128)(2,1)} %constant.7.clone.two, ...), custom_call_target="tpu_custom_call" | custom-call | tf_op jit(solution)/shard_map/pallas_call | solution.py:236
  30.8 1.3 %copy.10 = f32[3,2]{0,1:T(2,128)} copy(f32[3,2]{1,0:T(4,128)} %get-tuple-element.7) | data formatting | bytes 48
  32.0 1.3 %copy.12 = f32[3,512]{1,0:T(4,128)} copy(f32[3,512]{1,0:T(4,128)} %bitcast.15) | data formatting | bytes 12288

commit v2 on v1

--- a/solution.py
+++ b/solution.py
@@ -15,6 +15,7 @@
 CHIPS = 64
 PAIRS = ((0, 1), (0, 2), (1, 2))
 ROWS = 64
+GROUP = 3
 f32, bf16 = jnp.float32, jnp.bfloat16
 
 
@@ -39,17 +40,26 @@
     return one.astype(bf16), two.astype(bf16), turns
 
 
-def kernel(valid, strain, inter, notch, one, two, turns, out, board,
-           x, l1, l2, uv, it, nt, at, mid, y, part, num, came, send, recv, sc, sccame,
+def kernel(valid, strain, inter, notch, one, two, turns, out,
+           ok, x, l1, l2, uv, it, nt, at, mid, y, part, num, came, send, recv, sc, sccame,
            load_sem, x_sem, pair_sem, out_sem, in_sem):
     me = lax.axis_index("seg")
     chip, core = me // 2, lax.rem(me, 2)
     mate = me + 1 - 2 * core
 
     loads = [pltpu.make_async_copy(a, b, load_sem.at[n]) for n, (a, b) in enumerate(
-        ((inter, it.at[:, :3]), (notch, nt), (one, l1), (turns, uv), (two, l2)))]
-    takes = [pltpu.make_async_copy(strain.at[n], x.at[n], x_sem.at[n]) for n in range(18)]
-    for c in loads[:4] + takes + loads[4:]:
+        ((one, l1), (turns, uv), (two, l2), (inter, it.at[:, :3]), (notch, nt), (valid, ok)))]
+
+    def take(k):
+        part = pl.ds(k * GROUP, GROUP)
+        return pltpu.make_async_copy(strain.at[part], x.at[part], x_sem.at[k])
+
+    loads[0].start()
+    take(0).start()
+    loads[1].start()
+    for k in range(1, 18 // GROUP):
+        take(k).start()
+    for c in loads[2:]:
         c.start()
 
     barrier = pltpu.get_barrier_semaphore()
@@ -60,21 +70,14 @@
         to = lax.rem(chip + r, CHIPS) * 2 + core
         pl.semaphore_signal(barrier, inc=1, device_id=(to,), device_id_type=MESH)
 
+    for r in range(2):
+        send[0, pl.ds(6 + r, CHIPS, stride=8), :] = jnp.zeros((CHIPS, 128), f32)
+
+    even = (lax.broadcasted_iota(jnp.int16, (16, 128), 0) & 2) == 0
     loads[0].wait()
     loads[1].wait()
-    rows4 = it.reshape(2048, 128)
-    for h in range(2):
-        for w in range(2):
-            keep = [nt[pl.ds(2 * (2 * w + r) + h, CHIPS, stride=8), :].astype(f32) for r in range(2)]
-            for i in range(3):
-                got = [rows4[pl.ds(8 * (2 * w + r) + 4 * h + i, CHIPS, stride=32), :] * keep[r] for r in range(2)]
-                at[i, h, :, w * 128:(w + 1) * 128] = jnp.concatenate(got, axis=0).T
-
-    even = (lax.broadcasted_iota(jnp.int16, (16, 128), 0) & 2) == 0
-    loads[2].wait()
-    loads[3].wait()
-    for n in range(18):
-        takes[n].wait()
+
+    def one_transform(n):
         left, right = [], []
         for g in range(32):
             a, b = x[n, pl.ds(32 * g, 16), :], x[n, pl.ds(32 * g + 16, 16), :]
@@ -92,22 +95,40 @@
                 mid[n, h, pl.ds(16 * g, 16), :] = mr[:, 128 * h:128 * h + 128]
                 mid[n, 2 + h, pl.ds(16 * g, 16), :] = mi[:, 128 * h:128 * h + 128]
 
+    @pl.loop(0, 18 // GROUP)
+    def _(k):
+        take(k).wait()
+        for j in range(GROUP):
+            one_transform(k * GROUP + j)
+
+    loads[3].wait()
     loads[4].wait()
-    pl.semaphore_wait(barrier, CHIPS)
+    rows4 = it.reshape(2048, 128)
+
+    @pl.loop(0, 2)
+    def _(h):
+        for w in range(2):
+            keep = [nt[pl.ds(2 * (2 * w + r) + h, CHIPS, stride=8), :].astype(f32) for r in range(2)]
+            for i in range(3):
+                got = [rows4[pl.ds(8 * (2 * w + r) + 4 * h + i, CHIPS, stride=32), :] * keep[r] for r in range(2)]
+                at[i, h, :, w * 128:(w + 1) * 128] = jnp.concatenate(got, axis=0).T
+
+    loads[2].wait()
+    loads[5].wait()
 
     def second(block, s, slot):
-        rows = pl.ds(ROWS * block, ROWS)
+        rows = pl.ds(pl.multiple_of(ROWS * block, ROWS), ROWS)
         which = [d * 6 + s * 3 + t for t in range(3) for d in range(3)]
         data = jnp.concatenate(
             [jnp.concatenate([mid[n, k, rows, :] for n in which], axis=0) for k in range(4)], axis=1)
         table = jnp.concatenate([l2[k] for k in range(4)], axis=1)
         y[slot] = jnp.dot(data, table, preferred_element_type=f32)
 
-    signal = [jnp.zeros((8, 128), f32)] * 3
-    info = [jnp.zeros((8, 128), f32)] * 3
-
-    def stats(block, s, slot):
-        ok = valid[s].astype(f32)
+    zero = (jnp.zeros((8, 128), f32),) * 3
+
+    def stats(block, s, slot, signal, info):
+        signal, info = list(signal), list(info)
+        flag = ok[s].astype(f32)
         for g in range(ROWS // 8):
             for w in range(2):
                 lane = slice(128 * w, 128 * w + 128)
@@ -125,10 +146,10 @@
                         v = re[a] * re[b] + im[a] * im[b]
                         cross[i] = v if t == 0 else cross[i] + v
                 third = [p * (1.0 / 3.0) for p in power]
-                half, row = divmod(ROWS * block + 8 * g, 128)
-                row = pl.ds(row, 8)
+                half, row = block // 2, ROWS * (block % 2) + 8 * g
+                row = pl.ds(row if isinstance(row, int) else pl.multiple_of(row, 8), 8)
                 for i, (a, b) in enumerate(PAIRS):
-                    weight = ok / (third[a] * third[b])
+                    weight = flag / (third[a] * third[b])
                     v = weight * (cross[i] * (1.0 / 3.0))
                     f = at[i, half, row, lane]
                     signal[i] = signal[i] + f * v
@@ -137,6 +158,7 @@
                         part[i, half, row, lane] = v
                     else:
                         part[i, half, row, lane] = part[i, half, row, lane] + v
+        return tuple(signal), tuple(info)
 
     def pair(half):
         return pltpu.make_async_remote_copy(
@@ -165,15 +187,34 @@
                 send_sem=out_sem.at[half], recv_sem=in_sem.at[half],
                 device_id=(2 * to + core,), device_id_type=MESH).start()
 
-    order = [(block, s) for block in range(F // ROWS) for s in range(2)]
-    for n, (block, s) in enumerate(order):
-        second(block, s, n % 2)
-        if n:
-            stats(*order[n - 1], (n - 1) % 2)
-        if n == 5:
+    second(0, 0, 0)
+
+    def step(block, sums):
+        second(block, 1, 1)
+        sums = stats(block, 0, 0, *sums)
+        second(block + 1, 0, 0)
+        sums = stats(block, 1, 1, *sums)
+
+        @pl.when(block == 1)
+        def _():
             turn(0)
+            pl.semaphore_wait(barrier, CHIPS)
             pair(0).start()
-    stats(*order[-1], 1)
+
+        @pl.when(block == 2)
+        def _():
+            pair(0).wait()
+            merge(0)
+            spread(0)
+
+        return sums
+
+    sums = lax.fori_loop(0, F // ROWS - 1, step, (zero, zero))
+    last = F // ROWS - 1
+    second(last, 1, 1)
+    sums = stats(last, 0, 0, *sums)
+    sums = stats(last, 1, 1, *sums)
+    signal, info = map(list, sums)
     turn(1)
     rows = [jnp.sum(a, axis=0, keepdims=True) for a in signal + info]
     cells = [jnp.sum(a, axis=1, keepdims=True) for a in rows]
@@ -190,11 +231,6 @@
         device_id=(mate,), device_id_type=MESH)
     pair(1).start()
     scalars.start()
-    pair(0).wait()
-    for r in range(2):
-        send[0, pl.ds(6 + r, CHIPS, stride=8), :] = jnp.zeros((CHIPS, 128), f32)
-    merge(0)
-    spread(0)
     pair(1).wait()
     scalars.wait()
     both = sc[...] + sccame[...]
@@ -225,20 +261,26 @@
                 t = 2 * r + h
                 row = totals[h][2 * i + r:2 * i + r + 1]
                 out[t, i:i + 1] = kept[t:t + 1] * own[t, i:i + 1] * row / root
-        board[i:i + 1, 0:1] = sig / jnp.sqrt(inf)
-        board[i:i + 1, 1:2] = root
+        out[4, 0:1, i:i + 1] = sig / jnp.sqrt(inf)
+        out[4, 1:2, i:i + 1] = root
+
+
+def hand_on(result, out, board):
+    out[...] = result[0:4]
+    board[...] = result[4, 0:2, 0:3]
 
 
 def local(strain, valid, intersection, notch):
     one, two, turns = tables()
     strain = strain.reshape(18, 2, 512, 128).transpose(0, 2, 1, 3).reshape(18, 1024, 128)
     inter = intersection.reshape(3, 512, 128).transpose(1, 0, 2)
-    out, board = pl.pallas_call(
+    result = pl.pallas_call(
         kernel,
-        out_shape=(jax.ShapeDtypeStruct((4, 3, 128), f32), jax.ShapeDtypeStruct((3, 2), f32)),
-        in_specs=[pl.BlockSpec(memory_space=pltpu.SMEM)] + [pl.BlockSpec(memory_space=pl.ANY)] * 6,
-        out_specs=(pl.BlockSpec(memory_space=pltpu.VMEM), pl.BlockSpec(memory_space=pltpu.VMEM)),
+        out_shape=jax.ShapeDtypeStruct((5, 3, 128), f32),
+        in_specs=[pl.BlockSpec(memory_space=pl.ANY)] * 7,
+        out_specs=pl.BlockSpec(memory_space=pltpu.VMEM),
         scratch_shapes=[
+            pltpu.SMEM((2,), jnp.int32),
             pltpu.VMEM((18, 1024, 128), bf16),
             pltpu.VMEM((4, 512, 128), bf16),
             pltpu.VMEM((4, 512, 128), bf16),
@@ -255,16 +297,23 @@
             pltpu.VMEM((2, 8 * (CHIPS - 1), 128), f32),
             pltpu.VMEM((8, 128), f32),
             pltpu.VMEM((8, 128), f32),
-            pltpu.SemaphoreType.DMA((5,)),
+            pltpu.SemaphoreType.DMA((6,)),
             pltpu.SemaphoreType.DMA((18,)),
             pltpu.SemaphoreType.DMA((6,)),
             pltpu.SemaphoreType.DMA((2,)),
             pltpu.SemaphoreType.DMA((2,)),
         ],
         compiler_params=pltpu.CompilerParams(
-            collective_id=0, has_side_effects=True, vmem_limit_bytes=60 * 2**20),
-    )(valid, strain, inter, notch.reshape(512, 128), jnp.asarray(one), jnp.asarray(two), jnp.asarray(turns))
-    return out.transpose(1, 0, 2).reshape(3, 512), board
+            collective_id=0, has_side_effects=True, vmem_limit_bytes=40*2**20),
+    )(*(pltpu.with_memory_space_constraint(a, pltpu.HBM) for a in (valid, strain, inter, notch.reshape(512, 128), jnp.asarray(one), jnp.asarray(two), jnp.asarray(turns))))
+    out, board = pl.pallas_call(
+        hand_on,
+        out_shape=(jax.ShapeDtypeStruct((4, 3, 128), f32), jax.ShapeDtypeStruct((2, 3), f32)),
+        in_specs=[pl.BlockSpec(memory_space=pltpu.VMEM)],
+        out_specs=(pl.BlockSpec(memory_space=pltpu.VMEM), pl.BlockSpec(memory_space=pltpu.VMEM)),
+        compiler_params=pltpu.CompilerParams(vmem_limit_bytes=2**20),
+    )(result)
+    return out.transpose(1, 0, 2).reshape(3, 512), board.T
 
 
 def solution(mesh):

time: 33.6 us -> 26.2 us (0.78)
  Pallas kernels: 30.1 us -> 25.4 us
  local copies, waits for them, and re-layouts: 2.59 us -> 0 us
    pallas_call x1 -> x2, Pallas kernels: 30.1 us -> 25.4 us  [the longest x1 24.8 us: local(): pl.pallas_call(kernel, out_shape=jax.ShapeDtypeStruct((5, 3, 128), f32),...]
    unnamed x2 -> x0, local copies, waits for them, and re-layouts: 2.59 us -> none
where the time goes in v2:
time: 26.2 us; the launch traced here: 26 us
  Pallas kernels  25.4 us (97%)
  between operations  0.64 us (2%)
    pallas_call x1, Pallas kernels, local(): pl.pallas_call(kernel, out_shape=jax.ShapeDtypeStruct((5, 3, 128), f32),...  24.8 us
    pallas_call x1, Pallas kernels, local(): pl.pallas_call(hand_on, out_shape=(jax.ShapeDtypeStruct((4, 3, 128), f32)...  0.6 us

profile of v2, /device:TPU:1, one launch (start us, length us, event | category | flops | bytes accessed | tf_op | source)
XLA Modules:
  0.0 26.0 jit_solution(17239796798006184747)
XLA Ops:
  0.6 24.8 %shard_map.86.result = f32[5,3,128]{2,1,0:T(4,128)S(1)} custom-call(s32[2]{0:T(128)} %valid.1, bf16[18,1024,128]{2,1,0:T(8,128)(2,1)} %bitcast.13, f32[512,3,128]{2,1,0:T(4,128)} %bitcast.14, s32[512,128]{1,0:T(8,128)} %bitcast.15, bf16[4,512,128]{2,1,0:T(8,128)(2,1)} %constant.6.clone.one, bf16[4,512,128]{2,1,0:T(8,128)(2,1)} %constant.7.clone.two, ...), custom_call_target="tpu_custom_call" | custom-call | tf_op jit(solution)/shard_map/pallas_call | solution.py:277
  25.4 0.6 %shard_map.87 = (f32[4,3,128]{2,1,0:T(4,128)}, f32[2,3]{1,0:T(2,128)}) custom-call(f32[5,3,128]{2,1,0:T(4,128)S(1)} %shard_map.86.result), custom_call_target="tpu_custom_call" | custom-call | tf_op jit(solution)/shard_map/pallas_call | solution.py:309
